TPU v7x, 512 devices: a whole 4x8x8 slice. The times are simulated.
512 devices in a mesh: orb: 128 (over z, y, core), pair: 4 (over x).
Axes of the slice: x: 4, y: 8, z: 8, core: 2. Of those that a mesh axis runs over, the one named last changes fastest.
Arguments:
- orbitals: float32 [256, 32, 1024], P('orb'), may hold values from -6 to 6
- send_index: int32 [128, 4, 128], P('orb', 'pair'), may hold values from -1 to 1, as said below
- pair_left: int32 [128, 4, 128], P('orb', 'pair'), may hold values from -1 to 1, as said below
- pair_offset: int32 [128, 4, 128], P('orb', 'pair'), may hold values from -8 to 8
Outputs:
- exchange_field: float32 [256, 32, 1024], P('orb', 'pair')
Inputs may be any that keep to these rules, and one draw needn't show every extreme that they name: `send_index`: -1 marks an empty route. Toward some orb index, drawn from the seed, every route from every device is live. pair_left[d, p, s + c] is -1 exactly when send_index[s, p, d + c] is -1.
All inputs are finite; a program needn't handle non-finite values.
Results may differ from a plain program's by a relative error of at most 0.0075.
Values may be sent and summed in bfloat16 or wider, within the bound.
No kernel may reach another device: no remote copies, remote signals or barrier semaphores. Data moves between devices by JAX's collectives and lax.ppermute only.
A program may use at most 128 MiB of HBM per device.

v0:
```python
import jax
import jax.numpy as jnp
import numpy as np
from jax import lax
from jax.experimental import pallas as pl
from jax.experimental.pallas import tpu as pltpu
from jax.sharding import Mesh, PartitionSpec as P

FIELDS = 4
PAD = 8
UNROLL = 5
BUILD_STEP = 8
FINISH_STEP = 4
OWNER_BIT = 20
ENTRY_BITS = 7


def tile_kernel(side):
    blocks = side // 8
    pitch = side + PAD
    reach = FIELDS * pitch

    def kernel(core_ref, count_ref, code_ref, own_ref, peer_ref, out_ref, pairs, totals):
        lane = lax.broadcasted_iota(jnp.int32, (8, 128), 1)
        row = lax.broadcasted_iota(jnp.int32, (8, 128), 0)
        zero = jnp.zeros((8, 128), jnp.float32)
        keep_z = (lane % 32) < 31

        def boxes(ref, index, a, first):
            here = [
                ref[index, pl.ds(first + a * side + 8 * j, 8)].astype(jnp.float32)
                for j in range(blocks)
            ]
            edge = ref[index, pl.ds(first + 2 * side + 8 * a, 8)].astype(jnp.float32)
            turned = [pltpu.roll(v, 7, 0) for v in here] + [zero]
            up_x = [jnp.where(row < 7, turned[j], turned[j + 1]) for j in range(blocks)]
            up_y = []
            for j in range(blocks):
                shift = (96 - 32 * j) % 128
                beyond = pltpu.roll(edge, shift, 1) if shift else edge
                up_y.append(jnp.where(lane < 96, pltpu.roll(here[j], 96, 1), beyond))
            up_z = [pltpu.roll(v, 127, 1) for v in here]
            return here, up_x, up_y, up_z

        def build(step, _):
            for u in range(BUILD_STEP):
                peer = step * BUILD_STEP + u
                for a in range(2):
                    here, up_x, up_y, up_z = boxes(peer_ref, peer, a, 0)
                    base = pl.multiple_of((peer * 2 + a) * reach, 8)
                    for k, other in enumerate((here, up_x, up_y, up_z)):
                        pairs[pl.ds(base + k * pitch, 8)] = zero
                        for j in range(blocks):
                            pairs[pl.ds(base + k * pitch + PAD + 8 * j, 8)] = here[j] * other[j]
            return 0

        peers = peer_ref.shape[0]
        owners = own_ref.shape[0]
        entries = code_ref.shape[1]
        nothing = peers * 2 * reach
        lax.fori_loop(0, peers // BUILD_STEP, build, 0)
        for i in range(reach // 8):
            pairs[pl.ds(nothing + 8 * i, 8)] = zero

        def gather(own, _):
            for a in range(2):
                first = count_ref[own, 0] if a else jnp.int32(0)
                last = first + count_ref[own, a]

                def starts_of(g):
                    starts = []
                    for u in range(UNROLL):
                        index = first + g * UNROLL + u
                        code = code_ref[own, jnp.minimum(index, entries - 1)]
                        start = (code & ((1 << OWNER_BIT) - 1)) >> ENTRY_BITS
                        starts.append(jnp.where(index < last, start, nothing))
                    return starts

                def several(g, carried):
                    sums, starts = carried
                    following = starts_of(g + 1)
                    for start in starts:
                        sums = [
                            sums[k * blocks + j] + pairs[pl.ds(start + k * pitch + 8 * j, 8)]
                            for k in range(FIELDS)
                            for j in range(blocks)
                        ]
                    return sums, following

                groups = (last - first + UNROLL - 1) // UNROLL
                none = [zero] * (FIELDS * blocks)
                sums, _ = lax.fori_loop(0, groups, several, (none, starts_of(0)))
                for i, value in enumerate(sums):
                    totals[own, a, i] = value
            return 0

        lax.fori_loop(0, owners, gather, 0)

        slab = pl.multiple_of(core_ref[0] * (2 * side + 16), 16)

        def finish(step, _):
            for u in range(FINISH_STEP):
                own = step * FINISH_STEP + u
                edges = []
                for a in range(2):
                    here, up_x, up_y, up_z = boxes(own_ref, own, a, slab)
                    before = zero
                    for j in range(blocks):
                        self_sum, along_x, along_y, along_z = [
                            totals[own, a, k * blocks + j] for k in range(FIELDS)
                        ]
                        along_z = jnp.where(keep_z, along_z, 0.0)
                        back_x = pltpu.roll(here[j] * along_x, 1, 0)
                        back_y = pltpu.roll(here[j] * along_y, 32, 1)
                        back_z = pltpu.roll(here[j] * along_z, 1, 1)
                        total = up_x[j] * along_x + jnp.where(row > 0, back_x, before)
                        total = total + up_y[j] * along_y + jnp.where(lane >= 32, back_y, 0.0)
                        total = total + (up_z[j] * along_z + back_z)
                        before = back_x
                        total = (here[j] * self_sum + total / 6.0) / 6.0
                        chunk = own * blocks + j
                        out_ref[chunk, pl.ds(8 * a, 8)] = total.astype(out_ref.dtype)
                        if a == 0:
                            edges.append(back_y)
                        else:
                            both = jnp.where(lane < 32, edges[j], pltpu.roll(back_y, 32, 1))
                            out_ref[chunk, pl.ds(16, 8)] = (both / 36.0).astype(out_ref.dtype)
            return 0

        lax.fori_loop(0, owners // FINISH_STEP, finish, 0)

    return kernel


def apply_tile(core, counts, codes, own, peer, side, interpret=False):
    blocks = side // 8
    rows = (peer.shape[0] * 2 + 1) * FIELDS * (side + PAD)
    smem = pl.BlockSpec(memory_space=pltpu.SMEM)
    vmem = pl.BlockSpec(memory_space=pltpu.VMEM)
    return pl.pallas_call(
        tile_kernel(side),
        out_shape=jax.ShapeDtypeStruct((own.shape[0] * blocks, 24, 128), jnp.bfloat16),
        in_specs=[smem, smem, smem, vmem, vmem],
        out_specs=vmem,
        scratch_shapes=[
            pltpu.VMEM((rows, 128), jnp.float32),
            pltpu.VMEM((own.shape[0], 2, FIELDS * blocks, 8, 128), jnp.float32),
        ],
        compiler_params=pltpu.CompilerParams(vmem_limit_bytes=16 * 1024 * 1024),
        interpret=interpret,
    )(core, counts, codes, own, peer)


def tasks_of(own_meta, peer_meta, side):
    reach = FIELDS * (side + PAD)
    peers = own_meta.shape[2]
    base = jnp.arange(peers, dtype=jnp.int32)[None, :, None] * 2

    def keys(owner, partner, back):
        start = (base + partner) * reach + PAD - back
        return jnp.where(owner >= 0, (owner << OWNER_BIT) + (start << ENTRY_BITS), 4 << OWNER_BIT)

    as_left = keys(own_meta[1], peer_meta[0], own_meta[2])
    as_right = keys(own_meta[0], peer_meta[1], -peer_meta[2])
    owners = jnp.concatenate([own_meta[1], own_meta[0]], 1).reshape(own_meta.shape[1], -1)
    codes = jnp.concatenate([as_left, as_right], 1).reshape(own_meta.shape[1], -1)
    codes = codes + jnp.arange(codes.shape[1], dtype=jnp.int32)
    counts = jnp.stack([jnp.sum(owners == a, 1, dtype=jnp.int32) for a in range(2)], 1)
    rank = jnp.sum(codes[:, None, :] < codes[:, :, None], 2, dtype=jnp.int32)
    slot = jnp.arange(codes.shape[1], dtype=jnp.int32)
    placed = jnp.where(rank[:, None, :] == slot[None, :, None], codes[:, None, :], 0)
    return counts, jnp.sum(placed, 2, dtype=jnp.int32)


def payloads_of(rounded, meta, x):
    owned, side, _ = rounded.shape
    wide = jnp.pad(rounded, ((0, 0), (0, 0), (0, 128)))
    part = lax.dynamic_slice(wide, (0, 0, x * 256), (owned, side, 256 + side))

    def folded(edge):
        edge = edge.reshape(owned, side // 8, 8, side)
        return jnp.moveaxis(edge, 1, 2).reshape(owned * 8, 128)

    mains = [part[:, :, c * 128 : c * 128 + 128].reshape(owned * side, 128) for c in range(2)]
    edges = [folded(part[:, :, c * 128 + 128 : c * 128 + 128 + side]) for c in range(2)]
    peer = jnp.stack([jnp.concatenate([mains[c], edges[c], meta], 0) for c in range(2)])
    own = jnp.concatenate([mains[0], edges[0], mains[1], edges[1], meta], 0)
    return peer, own


def meta_of(received, kinds, pairs):
    first = received.shape[1] - 16
    meta = received[:, first : first + kinds * pairs].astype(jnp.int32)
    return meta.reshape(received.shape[0], pairs, kinds, 128)


def local(orbitals, send_index, pair_left, pair_offset):
    owned, side, width = orbitals.shape
    pairs = lax.axis_size("x")
    cores = lax.axis_size("c")
    z_size = lax.axis_size("z")
    y_size = lax.axis_size("y")
    x = lax.axis_index("x")
    y = lax.axis_index("y")
    z = lax.axis_index("z")
    rounded = orbitals.astype(jnp.bfloat16)
    meta = jnp.stack([send_index.reshape(-1), pair_left.reshape(-1), pair_offset.reshape(-1)])
    meta = jnp.broadcast_to(meta.astype(jnp.bfloat16)[None], (pairs, 3, 128))
    meta = lax.all_to_all(meta, "x", 0, 0, tiled=True).reshape(pairs * 3, 128)
    meta = jnp.pad(meta, ((0, 4), (0, 0)))
    payload, own_payload = payloads_of(rounded, meta, x)
    to_peers = jnp.broadcast_to(payload[None], (y_size,) + payload.shape)
    to_peers = to_peers.reshape((y_size * cores,) + payload.shape[1:])
    peer = lax.all_to_all(to_peers, ("y", "c"), 0, 0, tiled=True)
    own = lax.all_gather(own_payload, ("z", "c"), axis=0, tiled=False)

    own_meta = meta_of(own, 3, pairs)
    own_meta = lax.dynamic_slice_in_dim(own_meta, z * (y_size * cores), y_size * cores, 3)
    own_meta = jnp.transpose(own_meta, (2, 0, 3, 1))
    peer_meta = meta_of(peer, 3, pairs).reshape(-1, pairs, 3, z_size, y_size, cores)
    peer_meta = lax.dynamic_index_in_dim(peer_meta, y, 4, keepdims=False)
    peer_meta = peer_meta.reshape(-1, pairs, 3, z_size * cores)
    peer_meta = jnp.transpose(peer_meta, (2, 3, 0, 1))
    counts, codes = tasks_of(own_meta, peer_meta, side)

    core = lax.axis_index("c").astype(jnp.int32).reshape(1)
    partial = apply_tile(core, counts, codes, own, peer, side)
    landed = lax.all_to_all(partial, ("z", "c", "x"), 0, 0, tiled=True)
    landed = landed.reshape(z_size, cores, pairs, 24, 128).astype(jnp.float32)
    slabs = jnp.moveaxis(jnp.sum(landed, 0), 0, 1).reshape(cores * pairs, 24, 128)
    field = slabs[:, :16].reshape(cores * pairs, owned, 8, 128)
    edge = slabs[:-1, 16:, : owned * 32].reshape(-1, 8, owned, 32)
    edge = jnp.moveaxis(edge, 2, 1)
    field = field + jnp.pad(edge, ((1, 0), (0, 0), (0, 0), (0, 96)))
    field = -0.25 * field
    return jnp.transpose(field, (1, 2, 0, 3)).reshape(owned, 8, width)


def solution(mesh):
    fine = Mesh(np.asarray(mesh.devices).reshape(8, 8, 2, 4), ("z", "y", "c", "x"))
    orb = ("z", "y", "c")
    return jax.shard_map(
        local,
        mesh=fine,
        in_specs=(
            P(orb, None, None),
            P(orb, "x", None),
            P(orb, "x", None),
            P(orb, "x", None),
        ),
        out_specs=P(orb, "x", None),
        check_vma=False,
    )
```

profile of v0, /device:TPU:1, one launch (start us, length us, event | category | flops | bytes accessed | tf_op | source)
XLA Modules:
  0.0 75.6 jit_solution(18351844906770273730)
XLA Ops:
  0.0 0.0 copy-start
  0.0 0.0 copy-start.1
  0.0 0.7 convert_bitcast_fusion.2
  0.7 0.0 copy-done
  0.7 0.0 copy-done.1
  0.7 0.6 broadcast_in_dim.15
  1.3 4.8 %all-to-all-start = ((bf16[4,3,128]{2,1,0:T(4,128)(2,1)}), bf16[4,3,128]{2,1,0:T(4,128)(2,1)S(1)}, u32[]{:S(2)}, u32[]{:S(2)}) async-start(bf16[4,3,128]{2,1,0:T(4,128)(2,1)} %broadcast_in_dim.15), calls=%async_computation | async-start | bytes 8192 | tf_op jit(solution)/shard_map/all_to_all | solution.py:209
  6.1 1.0 %convert_element_type.33 = bf16[2,32,1024]{2,1,0:T(8,128)(2,1)S(1)} convert(f32[2,32,1024]{2,1,0:T(8,128)} %param.4) | non-fusion elementwise | flops 65536 | bytes 393216 | tf_op jit(solution)/shard_map/convert_element_type | solution.py:206
  7.2 0.1 fusion.20
  7.3 0.1 reshape.115
  7.4 0.1 reshape.112
  7.5 2.8 %all-to-all-done = bf16[4,3,128]{2,1,0:T(4,128)(2,1)S(1)} async-done(((bf16[4,3,128]{2,1,0:T(4,128)(2,1)}), bf16[4,3,128]{2,1,0:T(4,128)(2,1)S(1)}, u32[]{:S(2)}, u32[]{:S(2)}) %all-to-all-start) | async-done | bytes 3104 | tf_op jit(solution)/shard_map/all_to_all | solution.py:209
  10.3 0.8 %broadcast_in_dim.16 = bf16[8,2,96,128]{3,2,1,0:T(8,128)(2,1)} broadcast(bf16[2,96,128]{2,1,0:T(8,128)(2,1)S(1)} %pad_maximum_fusion), dimensions={1,2,3} | broadcast | bytes 442368 | tf_op jit(solution)/shard_map/broadcast_in_dim | solution.py:212
  11.1 9.7 %all-to-all-start.1 = ((bf16[16,96,128]{2,1,0:T(8,128)(2,1)}), bf16[16,96,128]{2,1,0:T(8,128)(2,1)S(1)}, u32[]{:S(2)}, u32[]{:S(2)}) async-start(bf16[16,96,128]{2,1,0:T(8,128)(2,1)} %bitcast.19), calls=%async_computation.1 | async-start | bytes 786432 | tf_op jit(solution)/shard_map/all_to_all | solution.py:214
  20.9 24.6 %all-gather = bf16[2816,128]{1,0:T(8,128)(2,1)S(1)} all-gather(bf16[176,128]{1,0:T(8,128)(2,1)S(1)} %get-tuple-element.18), channel_id=2, replica_groups=mesh['z'=8,'y'=8,'c'=2,'x'=4] {'z','c'}, dimensions={0}, use_global_device_ids=true | all-gather | bytes 765952 | tf_op jit(solution)/shard_map/all_gather | solution.py:215
  45.5 0.1 dynamic-slice_bitcast_fusion
  45.6 0.2 convert_reduce_fusion.3
  45.8 0.1 copy.76.count_ref
  45.9 0.0 all-to-all-done.1.peer_ref
  45.9 0.3 copy.71
  46.3 0.1 pad_add_fusion.1
  46.4 0.1 copy.73
  46.5 0.1 copy.74
  46.5 0.7 convert_reduce_fusion
  47.2 0.4 select_reduce_fusion.code_ref
  47.6 8.7 %shard_map.46 = bf16[64,24,128]{2,1,0:T(8,128)(2,1)S(1)} custom-call(s32[1]{0:T(128)} %bitcast.core_ref, s32[16,2]{1,0:T(8,128)S(1)} %copy.76.count_ref, s32[16,128]{1,0:T(8,128)S(1)} %select_reduce_fusion.code_ref, bf16[16,176,128]{2,1,0:T(8,128)(2,1)S(1)} %bitcast.109, bf16[16,96,128]{2,1,0:T(8,128)(2,1)S(1)} %all-to-all-done.1.peer_ref), custom_call_target="tpu_custom_call" | custom-call | tf_op jit(solution)/shard_map/pallas_call | solution.py:140
  56.4 18.3 %all_to_all.15 = bf16[64,24,128]{2,1,0:T(8,128)(2,1)S(1)} all-to-all(bf16[64,24,128]{2,1,0:T(8,128)(2,1)S(1)} %shard_map.46), channel_id=1, replica_groups=mesh['z'=8,'y'=8,'c'=2,'x'=4] {'z','c','x'}, dimensions={0} | all-to-all | bytes 786432 | tf_op jit(solution)/shard_map/all_to_all | solution.py:228
  74.7 0.1 convert_reduce_fusion.1
  74.8 0.1 reshape.124
  74.9 0.6 copy_bitcast_fusion.1
  (26 shorter events, 0.3 us)
Async XLA Ops:
  0.0 0.7 copy-start
  0.0 0.7 copy-start.1
  1.3 9.0 %all-to-all-start = ((bf16[4,3,128]{2,1,0:T(4,128)(2,1)}), bf16[4,3,128]{2,1,0:T(4,128)(2,1)S(1)}, u32[]{:S(2)}, u32[]{:S(2)}) async-start(bf16[4,3,128]{2,1,0:T(4,128)(2,1)} %broadcast_in_dim.15), calls=%async_computation | async-start | bytes 8192 | tf_op jit(solution)/shard_map/all_to_all | solution.py:209
  11.1 34.8 %all-to-all-start.1 = ((bf16[16,96,128]{2,1,0:T(8,128)(2,1)}), bf16[16,96,128]{2,1,0:T(8,128)(2,1)S(1)}, u32[]{:S(2)}, u32[]{:S(2)}) async-start(bf16[16,96,128]{2,1,0:T(8,128)(2,1)} %bitcast.19), calls=%async_computation.1 | async-start | bytes 786432 | tf_op jit(solution)/shard_map/all_to_all | solution.py:214
where the time goes:
time: 76.2 us; the launch traced here: 75.6 us
  blocking collectives  42.9 us (56%)
  starting transfers between devices  14.5 us (19%)
  Pallas kernels  8.74 us (11%)
  other arithmetic  3.82 us (5%)
  waiting for transfers between devices  2.79 us (4%)
  local copies, waits for them, and re-layouts  2.56 us (3%)
    all_gather x1, blocking collectives, local(): own = lax.all_gather(own_payload, ('z', 'c'), axis=0, tiled=False)  24.6 us
    all_to_all x1, blocking collectives, local(): landed = lax.all_to_all(partial, ('z', 'c', 'x'), 0, 0, tiled=True)  18.3 us
    all_to_all x1, starting transfers between devices, local(): peer = lax.all_to_all(to_peers, ('y', 'c'), 0, 0, tiled=True)  9.71 us
    pallas_call x1, Pallas kernels, apply_tile(): pl.pallas_call(tile_kernel(side), out_shape=jax.ShapeDtypeStruct((own.sha...  8.74 us
    all_to_all x1, starting transfers between devices, local(): meta = lax.all_to_all(meta, 'x', 0, 0, tiled=True).reshape(pairs * 3, 128)  4.83 us
    all_to_all x1, waiting for transfers between devices, local(): meta = lax.all_to_all(meta, 'x', 0, 0, tiled=True).reshape(pairs * 3, 128)  2.79 us
  transfers between devices with their start and end apart: 2, of which 1 were waited for; matrix products, arithmetic and copies ran while one was open for 2% of the time, Pallas kernels for 0%

commit v1 on v0

--- a/solution.py
+++ b/solution.py
@@ -8,8 +8,8 @@
 
 FIELDS = 4
 PAD = 8
-UNROLL = 5
-BUILD_STEP = 8
+UNROLL = 4
+BUILD_STEP = 4
 FINISH_STEP = 4
 OWNER_BIT = 20
 ENTRY_BITS = 7
@@ -205,9 +205,9 @@
     z = lax.axis_index("z")
     rounded = orbitals.astype(jnp.bfloat16)
     meta = jnp.stack([send_index.reshape(-1), pair_left.reshape(-1), pair_offset.reshape(-1)])
-    meta = jnp.broadcast_to(meta.astype(jnp.bfloat16)[None], (pairs, 3, 128))
+    meta = jnp.broadcast_to(meta[None], (pairs, 3, 128))
     meta = lax.all_to_all(meta, "x", 0, 0, tiled=True).reshape(pairs * 3, 128)
-    meta = jnp.pad(meta, ((0, 4), (0, 0)))
+    meta = jnp.pad(meta.astype(jnp.bfloat16), ((0, 4), (0, 0)))
     payload, own_payload = payloads_of(rounded, meta, x)
     to_peers = jnp.broadcast_to(payload[None], (y_size,) + payload.shape)
     to_peers = to_peers.reshape((y_size * cores,) + payload.shape[1:])

time: 76.2 us -> 76.4 us (level)
  no operation moved by 1% of the time
where the time goes in v1:
time: 76.4 us; the launch traced here: 75.7 us
  blocking collectives  42.8 us (56%)
  starting transfers between devices  14.5 us (19%)
  Pallas kernels  8.92 us (12%)
  local copies, waits for them, and re-layouts  3.25 us (4%)
  other arithmetic  3.13 us (4%)
  waiting for transfers between devices  2.81 us (4%)
    all_gather x1, blocking collectives, local(): own = lax.all_gather(own_payload, ('z', 'c'), axis=0, tiled=False)  24.6 us
    all_to_all x1, blocking collectives, local(): landed = lax.all_to_all(partial, ('z', 'c', 'x'), 0, 0, tiled=True)  18.3 us
    all_to_all x1, starting transfers between devices, local(): peer = lax.all_to_all(to_peers, ('y', 'c'), 0, 0, tiled=True)  9.72 us
    pallas_call x1, Pallas kernels, apply_tile(): pl.pallas_call(tile_kernel(side), out_shape=jax.ShapeDtypeStruct((own.sha...  8.92 us
    all_to_all x1, starting transfers between devices, local(): meta = lax.all_to_all(meta, 'x', 0, 0, tiled=True).reshape(pairs * 3, 128)  4.83 us
    all_to_all x1, waiting for transfers between devices, local(): meta = lax.all_to_all(meta, 'x', 0, 0, tiled=True).reshape(pairs * 3, 128)  2.81 us
  transfers between devices with their start and end apart: 2, of which 1 were waited for; matrix products, arithmetic and copies ran while one was open for 2% of the time, Pallas kernels for 0%

profile of v1, /device:TPU:1, one launch (start us, length us, event | category | flops | bytes accessed | tf_op | source)
XLA Modules:
  0.0 75.7 jit_solution(9166544093024070016)
XLA Ops:
  0.0 0.0 copy-start
  0.0 0.0 copy-start.1
  0.0 0.0 copy-start.2
  0.0 0.6 copy-done
  0.7 0.0 copy-done.1
  0.7 0.0 copy-done.2
  0.7 0.6 broadcast_in_dim.15
  1.3 4.8 %all-to-all-start = ((s32[4,3,128]{2,1,0:T(4,128)}), s32[4,3,128]{2,1,0:T(4,128)S(1)}, u32[]{:S(2)}, u32[]{:S(2)}) async-start(s32[4,3,128]{2,1,0:T(4,128)} %broadcast_in_dim.15), calls=%async_computation | async-start | bytes 16384 | tf_op jit(solution)/shard_map/all_to_all | solution.py:209
  6.1 1.0 %convert_element_type.34 = bf16[2,32,1024]{2,1,0:T(8,128)(2,1)S(1)} convert(f32[2,32,1024]{2,1,0:T(8,128)} %param.4) | non-fusion elementwise | flops 65536 | bytes 393216 | tf_op jit(solution)/shard_map/convert_element_type | solution.py:206
  7.1 0.1 fusion.20
  7.3 0.1 reshape.90
  7.3 0.1 reshape.87
  7.5 2.8 %all-to-all-done = s32[4,3,128]{2,1,0:T(4,128)S(1)} async-done(((s32[4,3,128]{2,1,0:T(4,128)}), s32[4,3,128]{2,1,0:T(4,128)S(1)}, u32[]{:S(2)}, u32[]{:S(2)}) %all-to-all-start) | async-done | bytes 6176 | tf_op jit(solution)/shard_map/all_to_all | solution.py:209
  10.4 0.8 %broadcast_in_dim.16 = bf16[8,2,96,128]{3,2,1,0:T(8,128)(2,1)} broadcast(bf16[2,96,128]{2,1,0:T(8,128)(2,1)S(1)} %pad_maximum_fusion), dimensions={1,2,3} | broadcast | bytes 442368 | tf_op jit(solution)/shard_map/broadcast_in_dim | solution.py:212
  11.2 9.7 %all-to-all-start.1 = ((bf16[16,96,128]{2,1,0:T(8,128)(2,1)}), bf16[16,96,128]{2,1,0:T(8,128)(2,1)S(1)}, u32[]{:S(2)}, u32[]{:S(2)}) async-start(bf16[16,96,128]{2,1,0:T(8,128)(2,1)} %bitcast.19), calls=%async_computation.1 | async-start | bytes 786432 | tf_op jit(solution)/shard_map/all_to_all | solution.py:214
  20.9 24.6 %all-gather = bf16[2816,128]{1,0:T(8,128)(2,1)S(1)} all-gather(bf16[176,128]{1,0:T(8,128)(2,1)S(1)} %get-tuple-element.18), channel_id=2, replica_groups=mesh['z'=8,'y'=8,'c'=2,'x'=4] {'z','c'}, dimensions={0}, use_global_device_ids=true | all-gather | bytes 765952 | tf_op jit(solution)/shard_map/all_gather | solution.py:215
  45.5 0.1 dynamic-slice_bitcast_fusion
  45.6 0.2 convert_reduce_fusion.3
  45.8 0.1 copy.76.count_ref
  45.9 0.0 all-to-all-done.1.peer_ref
  45.9 0.3 copy.71
  46.3 0.1 pad_add_fusion.1
  46.4 0.1 copy.73
  46.5 0.1 copy.74
  46.6 0.7 convert_reduce_fusion
  47.2 0.4 select_reduce_fusion.code_ref
  47.7 8.9 %shard_map.46 = bf16[64,24,128]{2,1,0:T(8,128)(2,1)S(1)} custom-call(s32[1]{0:T(128)} %bitcast.core_ref, s32[16,2]{1,0:T(8,128)S(1)} %copy.76.count_ref, s32[16,128]{1,0:T(8,128)S(1)} %select_reduce_fusion.code_ref, bf16[16,176,128]{2,1,0:T(8,128)(2,1)S(1)} %bitcast.106, bf16[16,96,128]{2,1,0:T(8,128)(2,1)S(1)} %all-to-all-done.1.peer_ref), custom_call_target="tpu_custom_call" | custom-call | tf_op jit(solution)/shard_map/pallas_call | solution.py:140
  56.6 18.3 %all_to_all.15 = bf16[64,24,128]{2,1,0:T(8,128)(2,1)S(1)} all-to-all(bf16[64,24,128]{2,1,0:T(8,128)(2,1)S(1)} %shard_map.46), channel_id=1, replica_groups=mesh['z'=8,'y'=8,'c'=2,'x'=4] {'z','c','x'}, dimensions={0} | all-to-all | bytes 786432 | tf_op jit(solution)/shard_map/all_to_all | solution.py:228
  74.9 0.1 convert_reduce_fusion.1
  74.9 0.1 reshape.98
  75.0 0.6 copy_bitcast_fusion.1
  (26 shorter events, 0.3 us)
Async XLA Ops:
  0.0 0.7 copy-start
  0.0 0.7 copy-start.1
  0.0 0.7 copy-start.2
  1.3 9.0 %all-to-all-start = ((s32[4,3,128]{2,1,0:T(4,128)}), s32[4,3,128]{2,1,0:T(4,128)S(1)}, u32[]{:S(2)}, u32[]{:S(2)}) async-start(s32[4,3,128]{2,1,0:T(4,128)} %broadcast_in_dim.15), calls=%async_computation | async-start | bytes 16384 | tf_op jit(solution)/shard_map/all_to_all | solution.py:209
  11.2 34.8 %all-to-all-start.1 = ((bf16[16,96,128]{2,1,0:T(8,128)(2,1)}), bf16[16,96,128]{2,1,0:T(8,128)(2,1)S(1)}, u32[]{:S(2)}, u32[]{:S(2)}) async-start(bf16[16,96,128]{2,1,0:T(8,128)(2,1)} %bitcast.19), calls=%async_computation.1 | async-start | bytes 786432 | tf_op jit(solution)/shard_map/all_to_all | solution.py:214
